TPU v7x, 128 devices: a whole 4x4x4 slice. The times are simulated.
128 devices in a mesh: wide: 16 (over x_hi, y, core), narrow: 8 (over z, x_lo).
Axes of the slice: x: 4 (x_hi: 2, x_lo: 2; x = x_hi * 2 + x_lo), y: 4, z: 4, core: 2. Of those that a mesh axis runs over, the one named last changes fastest.
Arguments:
- image: bfloat16 [2, 256, 256, 256], P(None, 'wide', 'narrow'), may hold values from -6 to 6
- deapodization: float32 [3, 256], replicated, may hold values from 0.5 to 2
- offsets: int32 [128, 16], P(('wide', 'narrow')), may hold values from 0 to 256
- cross_weight: bfloat16 [128, 16, 1536, 256], P(('wide', 'narrow')), may hold values from -0.375 to 0.375
- x_weight: bfloat16 [128, 16, 1536, 256], P(('wide', 'narrow')), may hold values from -0.375 to 0.375
Outputs:
- samples: float32 [128, 16, 2, 1536], P(('wide', 'narrow'))
Inputs may be any that keep to these rules, and one draw needn't show every extreme that they name: `offsets`: each entry is the first row, along the first frequency dimension, of a group's window of 256 rows in one slab.
All inputs are finite; a program needn't handle non-finite values.
Results may differ from a plain program's by a relative error of at most 0.007.
Values may be sent and summed in bfloat16 or wider, within the bound.
A program may use at most 128 MiB of HBM per device.

v0:
```python
import math

import jax
import jax.numpy as jnp
from jax import lax
from jax.sharding import PartitionSpec as P

G = 512
KZ = 64
BX = 256
SAMP = 1536


def shifted(block, axis, distance):
    devices = range(lax.axis_size(axis))
    route = [((i - distance) % len(devices), i) for i in devices]
    return lax.ppermute(block, axis, route)


def block_table(out_rows, inputs, grid_size, lowest):
    frequency = jnp.arange(out_rows, dtype=jnp.int32) + lowest
    position = jnp.arange(inputs, dtype=jnp.int32) - inputs // 2
    phases = jnp.mod(frequency[:, None] * position[None, :], grid_size)
    angles = phases.astype(jnp.float32) * (2.0 * math.pi / grid_size)
    factor = 1.0 / math.sqrt(inputs)
    cosine = (jnp.cos(angles) * factor).astype(jnp.bfloat16)
    sine = (jnp.sin(angles) * factor).astype(jnp.bfloat16)
    real_rows = jnp.stack([cosine, sine], axis=1)
    imag_rows = jnp.stack([-sine, cosine], axis=1)
    return jnp.stack([real_rows, imag_rows], axis=0)


def window_samples(window_rows, cross_rows, window_gain):
    partial_value = jnp.einsum(
        "ms,qcs->cmq", cross_rows, window_rows, preferred_element_type=jnp.float32
    )
    return jnp.sum(partial_value * window_gain.astype(jnp.float32)[None], axis=-1)


def per_device(image, deapodization, offsets, cross_weight, x_weight):
    wide_count = lax.axis_size("wide")
    wide_index = lax.axis_index("wide")
    narrow_index = lax.axis_index("narrow")
    block_x = image.shape[1]
    block_y = image.shape[2]
    image_width = image.shape[3]
    scale_x = lax.dynamic_slice_in_dim(deapodization[0], wide_index * block_x, block_x)
    scale_y = lax.dynamic_slice_in_dim(deapodization[1], narrow_index * block_y, block_y)
    weighted = (
        image.astype(jnp.float32)
        * scale_x[None, :, None, None]
        * scale_y[None, None, :, None]
        * deapodization[2][None, None, None, :]
    ).astype(jnp.bfloat16)
    z_table = block_table(KZ, image_width, G, -(KZ // 2))
    band_data = (
        jnp.einsum("okcz,cxyz->xyko", z_table, weighted, preferred_element_type=jnp.float32)
        .astype(jnp.bfloat16)
        .reshape(block_x, block_y, 2 * KZ)
    )
    line_table = block_table(G, image_width, G, -(G // 2))
    pieces = lax.all_to_all(band_data, "narrow", split_axis=2, concat_axis=1, tiled=True)
    item_count = pieces.shape[0]
    band_depth = pieces.shape[2] // 2
    unpacked = pieces.reshape(item_count, image_width, band_depth, 2)
    product = jnp.einsum(
        "oqcy,xykc->xoqk", line_table, unpacked, preferred_element_type=jnp.float32
    )
    columns = product.astype(jnp.bfloat16).reshape(item_count, 2, G * band_depth)
    slab_lines = lax.all_to_all(columns, "wide", split_axis=2, concat_axis=0, tiled=True)

    def transform_rows(table_rows, source):
        product = jnp.einsum(
            "opcx,xcs->pos", table_rows, source, preferred_element_type=jnp.float32
        )
        return product.astype(jnp.bfloat16)

    def slab_samples(slab_data, slab_index):
        start_row = lax.dynamic_index_in_dim(offsets[0], slab_index, 0, False)
        cross_rows = lax.dynamic_index_in_dim(cross_weight[0], slab_index, 0, False)
        window_gain = lax.dynamic_index_in_dim(x_weight[0], slab_index, 0, False)
        part_table = block_table(BX, image_width, G, start_row - G // 2)
        window_rows = transform_rows(part_table, slab_data)
        return window_samples(window_rows, cross_rows, window_gain)

    def record(results, slab_data, slab_index):
        return lax.dynamic_update_index_in_dim(
            results, slab_samples(slab_data, slab_index), slab_index, 0
        )

    results = jnp.zeros((wide_count, 2, SAMP), jnp.float32)

    def one_hop(hop_count, carried):
        current, results = carried
        incoming = shifted(current, "wide", 1)
        results = record(results, current, jnp.mod(wide_index - hop_count, wide_count))
        return (incoming, results)

    current, results = lax.fori_loop(0, wide_count - 1, one_hop, (slab_lines, results))
    results = record(results, current, jnp.mod(wide_index - (wide_count - 1), wide_count))
    return results[None]


def solution(mesh):
    return jax.shard_map(
        per_device,
        mesh=mesh,
        in_specs=(
            P(None, "wide", "narrow", None),
            P(),
            P(("wide", "narrow"), None),
            P(("wide", "narrow"), None, None, None),
            P(("wide", "narrow"), None, None, None),
        ),
        out_specs=P(("wide", "narrow"), None, None, None),
        check_vma=False,
    )
```

profile of v0, /device:TPU:0, one launch (start us, length us, event | category | flops | bytes accessed | tf_op | source)
XLA Modules:
  0.0 233.1 jit_solution(9781454502633909628)
XLA Ops:
  6.9 6.4 %all-to-all-start = ((bf16[8,2,4096]{2,1,0:T(2,128)(2,1)}), bf16[8,2,4096]{2,1,0:T(2,128)(2,1)S(1)}, u32[]{:S(2)}, u32[]{:S(2)}) async-start(bf16[8,2,4096]{2,1,0:T(2,128)(2,1)} %reshape.794), calls=%async_computation | async-start | bytes 262144 | tf_op jit(solution)/shard_map/all_to_all | solution.py:62
  13.3 2.5 %multiply_convert_fusion.3 = (bf16[512,1,256]{2,0,1:T(8,128)(2,1)S(1)}, bf16[512,1,256]{2,0,1:T(8,128)(2,1)S(1)}) fusion(s32[256]{0:T(256)S(1)} %get-tuple-element.280, s32[512]{0:T(512)S(1)} %iota_add_fusion.2), kind=kLoop, calls=%fused_computation.67 | loop fusion | flops 2359296 | bytes 527360 | tf_op jit(solution)/shard_map/convert_element_type | solution.py:27
  15.8 2.2 fusion.55
  23.8 1.7 copy.35
  25.4 18.1 %copy.65 = bf16[16,2,4096]{0,1,2:T(2,128)(2,1)} copy(bf16[16,2,4096]{0,2,1:T(8,128)(2,1)S(1)} %bitcast.158) | data formatting | bytes 524288 | tf_op jit(solution)/shard_map/reshape | solution.py:69
  43.6 7.3 %reshape.796 = bf16[16,2,4096]{2,1,0:T(2,128)(2,1)} reshape(bf16[4096,2,16]{2,1,0:T(2,128)(2,1)} %bitcast.159) | data formatting | bytes 524288
  50.9 6.9 %all-to-all-start.1 = ((bf16[16,2,4096]{2,1,0:T(2,128)(2,1)}), bf16[16,2,4096]{2,1,0:T(2,128)(2,1)S(1)}, u32[]{:S(2)}, u32[]{:S(2)}) async-start(bf16[16,2,4096]{2,1,0:T(2,128)(2,1)} %reshape.796), calls=%async_computation.1 | async-start | bytes 524288 | tf_op jit(solution)/shard_map/all_to_all | solution.py:70
  59.6 7.7 %all-to-all-done.1 = bf16[16,2,4096]{2,1,0:T(2,128)(2,1)S(1)} async-done(((bf16[16,2,4096]{2,1,0:T(2,128)(2,1)}), bf16[16,2,4096]{2,1,0:T(2,128)(2,1)S(1)}, u32[]{:S(2)}, u32[]{:S(2)}) %all-to-all-start.1) | async-done | bytes 262176 | tf_op jit(solution)/shard_map/all_to_all | solution.py:70
  68.7 3.2 %copy.57 = bf16[16,2,16,256]{3,0,2,1:T(8,128)(2,1)} copy(bf16[16,2,16,256]{0,1,3,2:T(2,128)(2,1)S(1)} %bitcast.157) | data formatting | bytes 524288 | tf_op jit(solution)/shard_map/all_to_all | solution.py:70
  72.7 157.0 %while.18 = (s32[]{:T(128)}, bf16[256,2,256]{2,0,1:T(8,128)(2,1)}, f32[16,2,1536]{2,1,0:T(2,128)}, s32[]{:T(128)}, s32[1,16]{1,0:T(1,128)S(1)}, /*index=5*/bf16[...) while((s32[]{:T(128)}, bf16[256,2,256]{2,0,1:T(8,128)(2,1)}, ...), condition=%wide.region_2.3_spmd, body=%wide.region_0.2_spmd.sunk | while | flops 541914624 | bytes 11577676 | solution.py:99
  78.8 2.1 fusion.81
  81.5 1.6 collective-permute-done
  89.3 2.1 fusion.81
  99.8 2.1 fusion.81
  110.2 2.1 fusion.81
  112.9 1.6 collective-permute-done
  120.7 2.1 fusion.81
  123.4 1.6 collective-permute-done
  131.2 2.1 fusion.81
  141.6 2.1 fusion.81
  152.1 2.1 fusion.81
  162.6 2.1 fusion.81
  173.0 2.1 fusion.81
  175.7 1.6 collective-permute-done
  183.5 2.1 fusion.81
  194.0 2.1 fusion.81
  204.4 2.1 fusion.81
  214.9 2.1 fusion.81
  217.6 1.6 collective-permute-done
  225.4 2.1 fusion.81
  228.1 1.6 collective-permute-done
  229.7 2.8 %fusion.22 = f32[2,1536]{1,0:T(2,128)S(1)} fusion(f32[1536,256]{0,1:T(8,128)} %copy.42, bf16[1,16,1536,256]{3,2,1,0:T(8,128)(2,1)} %get-tuple-element.372, s32[]{:T(128)S(6)} %select_n.179, bf16[1,256,2,256]{3,1,2,0:T(8,128)(2,1)} %get-tuple-element.267, bf16[1,256,2,256]{3,1,2,0:T(8,128)(2,1)S(1)} %get-tuple-element.266, ...), kind=kOutput, calls=%fused_computation.35 | convolution fusion | flops 539620352 | bytes 3158020 | tf_op jit(solution)/shard_map/ms,qcs->cmq/dot_general | solution.py:34
  (203 shorter events, 132.1 us)
Async XLA Ops:
  6.9 15.4 %all-to-all-start = ((bf16[8,2,4096]{2,1,0:T(2,128)(2,1)}), bf16[8,2,4096]{2,1,0:T(2,128)(2,1)S(1)}, u32[]{:S(2)}, u32[]{:S(2)}) async-start(bf16[8,2,4096]{2,1,0:T(2,128)(2,1)} %reshape.794), calls=%async_computation | async-start | bytes 262144 | tf_op jit(solution)/shard_map/all_to_all | solution.py:62
  50.9 21.8 %copy-start = (s32[1,16]{1,0:T(1,128)S(1)}, s32[1,16]{1,0:T(1,128)}, u32[]{:S(2)}) copy-start(s32[1,16]{1,0:T(1,128)} %param.9) | copy-start | bytes 196
  50.9 16.4 %all-to-all-start.1 = ((bf16[16,2,4096]{2,1,0:T(2,128)(2,1)}), bf16[16,2,4096]{2,1,0:T(2,128)(2,1)S(1)}, u32[]{:S(2)}, u32[]{:S(2)}) async-start(bf16[16,2,4096]{2,1,0:T(2,128)(2,1)} %reshape.796), calls=%async_computation.1 | async-start | bytes 524288 | tf_op jit(solution)/shard_map/all_to_all | solution.py:70
  73.6 9.5 %collective-permute-start = (bf16[256,2,256]{2,0,1:T(8,128)(2,1)S(1)}, bf16[256,2,256]{2,0,1:T(8,128)(2,1)}, u32[]{:S(2)}, u32[]{:S(2)}) collective-permute-start(bf16[256,2,256]{2,0,1:T(8,128)(2,1)S(1)} %copy.73), channel_id=1, source_target_pairs={{120,0},{0,8},{8,16},{16,24},{24,32},{32,40},{40,48},{48,56},{56,6... | collective-permute-start | bytes 786440 | tf_op jit(solution)/shard_map/while/body/eval_jaxpr/ppermute | solution.py:17
  84.1 9.5 %collective-permute-start = (bf16[256,2,256]{2,0,1:T(8,128)(2,1)S(1)}, bf16[256,2,256]{2,0,1:T(8,128)(2,1)}, u32[]{:S(2)}, u32[]{:S(2)}) collective-permute-start(bf16[256,2,256]{2,0,1:T(8,128)(2,1)S(1)} %copy.73), channel_id=1, source_target_pairs={{120,0},{0,8},{8,16},{16,24},{24,32},{32,40},{40,48},{48,56},{56,6... | collective-permute-start | bytes 786440 | tf_op jit(solution)/shard_map/while/body/eval_jaxpr/ppermute | solution.py:17
  94.6 9.5 %collective-permute-start = (bf16[256,2,256]{2,0,1:T(8,128)(2,1)S(1)}, bf16[256,2,256]{2,0,1:T(8,128)(2,1)}, u32[]{:S(2)}, u32[]{:S(2)}) collective-permute-start(bf16[256,2,256]{2,0,1:T(8,128)(2,1)S(1)} %copy.73), channel_id=1, source_target_pairs={{120,0},{0,8},{8,16},{16,24},{24,32},{32,40},{40,48},{48,56},{56,6... | collective-permute-start | bytes 786440 | tf_op jit(solution)/shard_map/while/body/eval_jaxpr/ppermute | solution.py:17
  105.0 9.5 %collective-permute-start = (bf16[256,2,256]{2,0,1:T(8,128)(2,1)S(1)}, bf16[256,2,256]{2,0,1:T(8,128)(2,1)}, u32[]{:S(2)}, u32[]{:S(2)}) collective-permute-start(bf16[256,2,256]{2,0,1:T(8,128)(2,1)S(1)} %copy.73), channel_id=1, source_target_pairs={{120,0},{0,8},{8,16},{16,24},{24,32},{32,40},{40,48},{48,56},{56,6... | collective-permute-start | bytes 786440 | tf_op jit(solution)/shard_map/while/body/eval_jaxpr/ppermute | solution.py:17
  115.5 9.5 %collective-permute-start = (bf16[256,2,256]{2,0,1:T(8,128)(2,1)S(1)}, bf16[256,2,256]{2,0,1:T(8,128)(2,1)}, u32[]{:S(2)}, u32[]{:S(2)}) collective-permute-start(bf16[256,2,256]{2,0,1:T(8,128)(2,1)S(1)} %copy.73), channel_id=1, source_target_pairs={{120,0},{0,8},{8,16},{16,24},{24,32},{32,40},{40,48},{48,56},{56,6... | collective-permute-start | bytes 786440 | tf_op jit(solution)/shard_map/while/body/eval_jaxpr/ppermute | solution.py:17
  126.0 9.5 %collective-permute-start = (bf16[256,2,256]{2,0,1:T(8,128)(2,1)S(1)}, bf16[256,2,256]{2,0,1:T(8,128)(2,1)}, u32[]{:S(2)}, u32[]{:S(2)}) collective-permute-start(bf16[256,2,256]{2,0,1:T(8,128)(2,1)S(1)} %copy.73), channel_id=1, source_target_pairs={{120,0},{0,8},{8,16},{16,24},{24,32},{32,40},{40,48},{48,56},{56,6... | collective-permute-start | bytes 786440 | tf_op jit(solution)/shard_map/while/body/eval_jaxpr/ppermute | solution.py:17
  136.5 9.5 %collective-permute-start = (bf16[256,2,256]{2,0,1:T(8,128)(2,1)S(1)}, bf16[256,2,256]{2,0,1:T(8,128)(2,1)}, u32[]{:S(2)}, u32[]{:S(2)}) collective-permute-start(bf16[256,2,256]{2,0,1:T(8,128)(2,1)S(1)} %copy.73), channel_id=1, source_target_pairs={{120,0},{0,8},{8,16},{16,24},{24,32},{32,40},{40,48},{48,56},{56,6... | collective-permute-start | bytes 786440 | tf_op jit(solution)/shard_map/while/body/eval_jaxpr/ppermute | solution.py:17
  146.9 9.5 %collective-permute-start = (bf16[256,2,256]{2,0,1:T(8,128)(2,1)S(1)}, bf16[256,2,256]{2,0,1:T(8,128)(2,1)}, u32[]{:S(2)}, u32[]{:S(2)}) collective-permute-start(bf16[256,2,256]{2,0,1:T(8,128)(2,1)S(1)} %copy.73), channel_id=1, source_target_pairs={{120,0},{0,8},{8,16},{16,24},{24,32},{32,40},{40,48},{48,56},{56,6... | collective-permute-start | bytes 786440 | tf_op jit(solution)/shard_map/while/body/eval_jaxpr/ppermute | solution.py:17
  157.4 9.5 %collective-permute-start = (bf16[256,2,256]{2,0,1:T(8,128)(2,1)S(1)}, bf16[256,2,256]{2,0,1:T(8,128)(2,1)}, u32[]{:S(2)}, u32[]{:S(2)}) collective-permute-start(bf16[256,2,256]{2,0,1:T(8,128)(2,1)S(1)} %copy.73), channel_id=1, source_target_pairs={{120,0},{0,8},{8,16},{16,24},{24,32},{32,40},{40,48},{48,56},{56,6... | collective-permute-start | bytes 786440 | tf_op jit(solution)/shard_map/while/body/eval_jaxpr/ppermute | solution.py:17
  167.9 9.5 %collective-permute-start = (bf16[256,2,256]{2,0,1:T(8,128)(2,1)S(1)}, bf16[256,2,256]{2,0,1:T(8,128)(2,1)}, u32[]{:S(2)}, u32[]{:S(2)}) collective-permute-start(bf16[256,2,256]{2,0,1:T(8,128)(2,1)S(1)} %copy.73), channel_id=1, source_target_pairs={{120,0},{0,8},{8,16},{16,24},{24,32},{32,40},{40,48},{48,56},{56,6... | collective-permute-start | bytes 786440 | tf_op jit(solution)/shard_map/while/body/eval_jaxpr/ppermute | solution.py:17
  178.3 9.5 %collective-permute-start = (bf16[256,2,256]{2,0,1:T(8,128)(2,1)S(1)}, bf16[256,2,256]{2,0,1:T(8,128)(2,1)}, u32[]{:S(2)}, u32[]{:S(2)}) collective-permute-start(bf16[256,2,256]{2,0,1:T(8,128)(2,1)S(1)} %copy.73), channel_id=1, source_target_pairs={{120,0},{0,8},{8,16},{16,24},{24,32},{32,40},{40,48},{48,56},{56,6... | collective-permute-start | bytes 786440 | tf_op jit(solution)/shard_map/while/body/eval_jaxpr/ppermute | solution.py:17
  188.8 9.5 %collective-permute-start = (bf16[256,2,256]{2,0,1:T(8,128)(2,1)S(1)}, bf16[256,2,256]{2,0,1:T(8,128)(2,1)}, u32[]{:S(2)}, u32[]{:S(2)}) collective-permute-start(bf16[256,2,256]{2,0,1:T(8,128)(2,1)S(1)} %copy.73), channel_id=1, source_target_pairs={{120,0},{0,8},{8,16},{16,24},{24,32},{32,40},{40,48},{48,56},{56,6... | collective-permute-start | bytes 786440 | tf_op jit(solution)/shard_map/while/body/eval_jaxpr/ppermute | solution.py:17
  199.3 9.5 %collective-permute-start = (bf16[256,2,256]{2,0,1:T(8,128)(2,1)S(1)}, bf16[256,2,256]{2,0,1:T(8,128)(2,1)}, u32[]{:S(2)}, u32[]{:S(2)}) collective-permute-start(bf16[256,2,256]{2,0,1:T(8,128)(2,1)S(1)} %copy.73), channel_id=1, source_target_pairs={{120,0},{0,8},{8,16},{16,24},{24,32},{32,40},{40,48},{48,56},{56,6... | collective-permute-start | bytes 786440 | tf_op jit(solution)/shard_map/while/body/eval_jaxpr/ppermute | solution.py:17
  209.7 9.5 %collective-permute-start = (bf16[256,2,256]{2,0,1:T(8,128)(2,1)S(1)}, bf16[256,2,256]{2,0,1:T(8,128)(2,1)}, u32[]{:S(2)}, u32[]{:S(2)}) collective-permute-start(bf16[256,2,256]{2,0,1:T(8,128)(2,1)S(1)} %copy.73), channel_id=1, source_target_pairs={{120,0},{0,8},{8,16},{16,24},{24,32},{32,40},{40,48},{48,56},{56,6... | collective-permute-start | bytes 786440 | tf_op jit(solution)/shard_map/while/body/eval_jaxpr/ppermute | solution.py:17
  220.2 9.5 %collective-permute-start = (bf16[256,2,256]{2,0,1:T(8,128)(2,1)S(1)}, bf16[256,2,256]{2,0,1:T(8,128)(2,1)}, u32[]{:S(2)}, u32[]{:S(2)}) collective-permute-start(bf16[256,2,256]{2,0,1:T(8,128)(2,1)S(1)} %copy.73), channel_id=1, source_target_pairs={{120,0},{0,8},{8,16},{16,24},{24,32},{32,40},{40,48},{48,56},{56,6... | collective-permute-start | bytes 786440 | tf_op jit(solution)/shard_map/while/body/eval_jaxpr/ppermute | solution.py:17
where the time goes:
time: 235 us; the launch traced here: 233 us
  local copies, waits for them, and re-layouts  83.9 us (36%)
  other arithmetic  66.6 us (28%)
  matrix products  36 us (15%)
  waiting for transfers between devices  32.3 us (14%)
  starting transfers between devices  13.3 us (6%)
    dot_general x16, matrix products, window_samples(): jnp.einsum('ms,qcs->cmq', cross_rows, window_rows, preferred_element_type...  34.1 us
    ppermute x15, waiting for transfers between devices, shifted(): return lax.ppermute(block, axis, route)  24.6 us
    convert_element_type x18, other arithmetic, block_table(): sine = (jnp.sin(angles) * factor).astype(jnp.bfloat16)  23.3 us
    dynamic_slice x30, local copies, waits for them, and re-layouts, slab_samples(): window_gain = lax.dynamic_index_in_dim(x_weight[0], slab_index, 0, False)  22 us
    neg x18, other arithmetic, block_table(): imag_rows = jnp.stack([-sine, cosine], axis=1)  19.6 us
    reshape x1, local copies, waits for them, and re-layouts, per_device(): product.astype(jnp.bfloat16).reshape(item_count, 2, G * band_depth)  18.1 us
    another operation x15, local copies, waits for them, and re-layouts  14.3 us
    unnamed x6, local copies, waits for them, and re-layouts  10.2 us
  transfers between devices with their start and end apart: 17, of which 16 were waited for; matrix products, arithmetic and copies ran while one was open for 55% of the time, Pallas kernels for 0%

commit v1 on v0

v1 whole, which is shorter than its diff:
```python
import functools
import math

import jax
import jax.numpy as jnp
import ml_dtypes
import numpy as np
from jax import lax
from jax.experimental import pallas as pl
from jax.experimental.pallas import tpu as pltpu
from jax.sharding import PartitionSpec as P

F32 = jnp.float32
BF16 = jnp.bfloat16
MESH = pl.DeviceIdType.MESH
NT = (((1,), (1,)), ((), ()))
NN = (((1,), (0,)), ((), ()))


def trig(frequency, position):
    phase = np.mod(frequency[:, None] * position[None, :], 512)
    angle = phase * (2.0 * math.pi / 512)
    scale = 1.0 / math.sqrt(256)
    return np.cos(angle) * scale, np.sin(angle) * scale


def tables():
    position = np.arange(256) - 128
    cosine, sine = trig(np.arange(64) - 32, position)
    tz = np.zeros((2, 256, 8, 2, 8), np.float32)
    cos_t = cosine.reshape(8, 8, 256).transpose(2, 1, 0)
    sin_t = sine.reshape(8, 8, 256).transpose(2, 1, 0)
    tz[0, :, :, 0], tz[1, :, :, 0] = cos_t, sin_t
    tz[0, :, :, 1], tz[1, :, :, 1] = -sin_t, cos_t
    tz = tz.reshape(2, 256, 128)
    cosine, sine = trig(np.arange(512) - 256, position)
    ty = np.stack([cosine, sine])
    tx = ty[:, :256].reshape(2, 256, 2, 4, 2, 16).transpose(0, 1, 4, 2, 3, 5).reshape(2, 256, 256)
    return tz.astype(ml_dtypes.bfloat16), ty.astype(ml_dtypes.bfloat16), tx.astype(np.float32)


def kernel(
    img_h, deap, deap_s, off_s, cw_h, xw_h, tz_h, ty_h, tx_h, out,
    img, tz, ty, tx, dyz, send, blk, band, tyf, twin, col, cw, xw, xwt, win_a, win_b,
    in_sem, cw_sem, xw_sem, s1, r1, s2, r2, s3, r3,
):
    wide = lax.axis_index("wide")
    narrow = lax.axis_index("narrow")
    xh = wide // 8
    y = (wide // 2) % 4
    core = wide % 2
    me = xh * 8 + narrow

    def at_y(step):
        return {"wide": xh * 8 + ((y + step) % 4) * 2 + core, "narrow": narrow}

    other = {"wide": xh * 8 + y * 2 + (1 - core), "narrow": narrow}

    def peer(d):
        return {"wide": (d // 8) * 8 + y * 2 + core, "narrow": d % 8}

    ins = [
        pltpu.make_async_copy(img_h, img, in_sem.at[0]),
        pltpu.make_async_copy(tz_h, tz, in_sem.at[1]),
        pltpu.make_async_copy(ty_h, ty, in_sem.at[2]),
        pltpu.make_async_copy(tx_h, tx, in_sem.at[3]),
    ]
    for copy in ins:
        copy.start()

    def xw_copy(s):
        return pltpu.make_async_copy(xw_h.at[s], xw.at[s], xw_sem.at[s])

    def cw_copy(s):
        return pltpu.make_async_copy(cw_h.at[s], cw.at[s], cw_sem.at[s])

    barrier = pltpu.get_barrier_semaphore()

    def greet(i, _):
        pl.semaphore_signal(barrier, inc=1, device_id=peer((me + i) % 16), device_id_type=MESH)
        return 0

    lax.fori_loop(1, 16, greet, 0)
    for target in (at_y(1), at_y(3), other):
        pl.semaphore_signal(barrier, inc=1, device_id=target, device_id_type=MESH)

    dz = deap[2:3, :]
    for i in range(32):
        dyz[i : i + 1, :] = dz * deap_s[1, narrow * 32 + i]
    ins[0].wait()
    for x in range(16):
        gain = dyz[...] * deap_s[0, wide * 16 + x]
        for c in range(2):
            img[c, x] = (img[c, x].astype(F32) * gain).astype(BF16)
    ins[1].wait()
    freq = lax.dot_general(img[0].reshape(512, 256), tz[0], NN, preferred_element_type=F32)
    freq += lax.dot_general(img[1].reshape(512, 256), tz[1], NN, preferred_element_type=F32)
    lane = lax.broadcasted_iota(jnp.int32, (32, 128), 1)
    parts = [freq[x * 32 : (x + 1) * 32] for x in range(16)]
    for b in range(4):
        step = 1 << b
        low = (lane & step) == 0
        for x in range(16):
            if x & step:
                continue
            a0, a1 = parts[x], parts[x + step]
            parts[x] = jnp.where(low, a0, pltpu.roll(a1, step, 1))
            parts[x + step] = jnp.where(low, pltpu.roll(a0, 128 - step, 1), a1)
    for n in range(8):
        for c in range(2):
            send[n, c] = parts[c * 8 + n].astype(BF16)

    def start_xw(s, _):
        xw_copy(s).start()
        return 0

    def start_cw(s, _):
        cw_copy(s).start()
        return 0

    lax.fori_loop(0, 16, start_xw, 0)
    lax.fori_loop(0, 16, start_cw, 0)

    pl.semaphore_wait(barrier, 18)

    def piece(d, src):
        return pltpu.make_async_remote_copy(
            src_ref=send.at[d % 8],
            dst_ref=blk.at[src // 8, :, pl.ds(pl.multiple_of((src % 8) * 32, 32), 32), :],
            send_sem=s1.at[d],
            recv_sem=r1.at[src],
            device_id=peer(d),
            device_id_type=MESH,
        )

    def send_piece(i, _):
        piece((me + i) % 16, me).start()
        return 0

    lax.fori_loop(1, 16, send_piece, 0)
    blk[xh, :, pl.ds(pl.multiple_of(narrow * 32, 32), 32), :] = send[narrow]

    ins[2].wait()
    tyf[0, :, 0:256] = ty[0]
    tyf[0, :, 256:512] = ty[1]
    tyf[1, :, 0:256] = -ty[1]
    tyf[1, :, 256:512] = ty[0]
    ins[3].wait()

    place = lax.broadcasted_iota(jnp.int32, (8, 256), 1)
    place = (
        ((place >> 6) & 1) * 128 + ((place >> 4) & 3) * 32 + (place >> 7) * 16 + (place & 15) - 128
    )

    def windows(s, _):
        phase = (place * off_s[0, s]) & 511
        angle = phase.astype(F32) * (2.0 * math.pi / 512)
        cosine, sine = jnp.cos(angle)[0:1], jnp.sin(angle)[0:1]
        twin[s, 0] = (tx[0] * cosine - tx[1] * sine).astype(BF16)
        twin[s, 1] = (tx[1] * cosine + tx[0] * sine).astype(BF16)
        return 0

    lax.fori_loop(0, 16, windows, 0)

    def transpose_slabs(first, last):
        def one(s, _):
            xw_copy(s).wait()
            for j in range(6):
                xwt[s, j] = xw[s, j * 256 : (j + 1) * 256, :].T
            return 0

        lax.fori_loop(first, last, one, 0)

    def got_piece(i, _):
        piece(me, (me + i) % 16).wait_recv()
        return 0

    lax.fori_loop(1, 16, got_piece, 0)

    b0, b1 = blk[0].reshape(512, 128), blk[1].reshape(512, 128)
    band[0, y, core] = jnp.concatenate([b0[:, :64], b1[:, :64]], axis=1)
    band[1, y, core] = jnp.concatenate([b0[:, 64:], b1[:, 64:]], axis=1)

    def ring(kg, kind, slot, step):
        return pltpu.make_async_remote_copy(
            src_ref=band.at[kg, (y + slot) % 4, core],
            dst_ref=band.at[kg, (y + slot) % 4, core],
            send_sem=s2.at[kg, kind],
            recv_sem=r2.at[kg, kind],
            device_id=at_y(step),
            device_id_type=MESH,
        )

    def got_ring(kg, kind, slot):
        return pltpu.make_async_remote_copy(
            src_ref=band.at[kg, (y + slot) % 4, core],
            dst_ref=band.at[kg, (y + slot) % 4, core],
            send_sem=s2.at[kg, kind],
            recv_sem=r2.at[kg, kind],
            device_id=at_y(1),
            device_id_type=MESH,
        )

    def across(kg, slot, side):
        return pltpu.make_async_remote_copy(
            src_ref=band.at[kg, (y + slot) % 4, side],
            dst_ref=band.at[kg, (y + slot) % 4, side],
            send_sem=s3.at[kg, slot],
            recv_sem=r3.at[kg, slot],
            device_id=other,
            device_id_type=MESH,
        )

    ring(0, 0, 0, 1).start()
    ring(0, 1, 0, 3).start()
    ring(1, 1, 0, 3).start()
    across(0, 0, core).start()
    across(1, 0, core).start()

    transpose_slabs(0, 5)

    got_ring(0, 0, 3).wait_recv()
    ring(0, 2, 3, 1).start()
    ring(1, 0, 0, 1).start()
    across(0, 3, core).start()
    got_ring(0, 1, 1).wait_recv()
    across(0, 1, core).start()

    transpose_slabs(5, 11)

    got_ring(1, 1, 1).wait_recv()
    ring(1, 2, 1, 3).start()
    across(1, 1, core).start()
    got_ring(0, 2, 2).wait_recv()
    across(0, 2, core).start()

    transpose_slabs(11, 16)

    got_ring(1, 0, 3).wait_recv()
    across(1, 3, core).start()

    def lines(kg):
        lane_b = lax.broadcasted_iota(jnp.int32, (512, 128), 1)
        sides = []
        for side in range(2):
            rows = [band[kg, i, side].astype(F32) for i in range(4)]
            for b in range(2):
                step, shift = 1 << b, 16 << b
                low = (lane_b & shift) == 0
                for i in range(4):
                    if i & step:
                        continue
                    a0, a1 = rows[i], rows[i + step]
                    rows[i] = jnp.where(low, a0, pltpu.roll(a1, shift, 1))
                    rows[i + step] = jnp.where(low, pltpu.roll(a0, 128 - shift, 1), a1)
            sides.append([r.astype(BF16) for r in rows])
        for k in range(4):
            data = jnp.concatenate([sides[0][k], sides[1][k]], axis=1)
            for c in range(2):
                line = lax.dot_general(tyf[c], data, NN, preferred_element_type=F32)
                for s in range(16):
                    for t in range(2):
                        col[s, c, t, pl.ds(kg * 4 + k, 32, stride=8), :] = line[
                            s * 32 : (s + 1) * 32, t * 128 : (t + 1) * 128
                        ]

    for slot in range(4):
        across(0, slot, 1 - core).wait_recv()
    lines(0)
    got_ring(1, 2, 2).wait_recv()
    across(1, 2, core).start()
    for slot in range(4):
        across(1, slot, 1 - core).wait_recv()
    lines(1)

    def got_cw(s, _):
        cw_copy(s).wait()
        return 0

    lax.fori_loop(0, 16, got_cw, 0)

    def to_window(s, win):
        cosine, sine = twin[s, 0], twin[s, 1]
        real = jnp.concatenate([cosine, sine], axis=1)
        imag = jnp.concatenate([-sine, cosine], axis=1)
        source = jnp.concatenate(
            [col[s, c, t].astype(BF16) for c in range(2) for t in range(2)], axis=1
        )
        win[0:256] = lax.dot_general(real, source, NT, preferred_element_type=F32).astype(BF16)
        win[256:512] = lax.dot_general(imag, source, NT, preferred_element_type=F32).astype(BF16)

    def to_samples(s, win):
        for j in range(6):
            rows = cw[s, j * 256 : (j + 1) * 256, :]
            part = lax.dot_general(win[...], rows, NT, preferred_element_type=F32)
            gain = xwt[s, j].astype(F32)
            here = slice(j * 256, (j + 1) * 256)
            out[s, 0:1, here] = jnp.sum(part[:256] * gain, axis=0, keepdims=True)
            out[s, 1:2, here] = jnp.sum(part[256:] * gain, axis=0, keepdims=True)

    to_window(0, win_a)

    def pair(i, _):
        s = i * 2
        to_window(s + 1, win_b)
        to_samples(s, win_a)
        to_window((s + 2) % 16, win_a)
        to_samples(s + 1, win_b)
        return 0

    lax.fori_loop(0, 8, pair, 0)

    def sent(i, _):
        piece((me + i) % 16, me).wait_send()
        return 0

    lax.fori_loop(1, 16, sent, 0)
    for kg in range(2):
        ring(kg, 0, 0, 1).wait_send()
        ring(kg, 1, 0, 3).wait_send()
        for slot in range(4):
            across(kg, slot, core).wait_send()
    ring(0, 2, 3, 1).wait_send()
    ring(1, 2, 1, 3).wait_send()


def per_device(image, deapodization, offsets, cross_weight, x_weight):
    tz, ty, tx = (jnp.asarray(t) for t in tables())
    any_space = pl.BlockSpec(memory_space=pl.ANY)
    smem = pl.BlockSpec(memory_space=pltpu.SMEM)
    vmem = pl.BlockSpec(memory_space=pltpu.VMEM)
    dma = pltpu.SemaphoreType.DMA
    samples = pl.pallas_call(
        kernel,
        out_shape=jax.ShapeDtypeStruct((16, 2, 1536), F32),
        in_specs=[any_space, vmem, smem, smem] + [any_space] * 5,
        out_specs=vmem,
        scratch_shapes=[
            pltpu.VMEM((2, 16, 32, 256), BF16),
            pltpu.VMEM((2, 256, 128), BF16),
            pltpu.VMEM((2, 512, 256), BF16),
            pltpu.VMEM((2, 256, 256), F32),
            pltpu.VMEM((32, 256), F32),
            pltpu.VMEM((8, 2, 32, 128), BF16),
            pltpu.VMEM((2, 2, 256, 128), BF16),
            pltpu.VMEM((2, 4, 2, 512, 128), BF16),
            pltpu.VMEM((2, 512, 512), BF16),
            pltpu.VMEM((16, 2, 256, 256), BF16),
            pltpu.VMEM((16, 2, 2, 256, 128), F32),
            pltpu.VMEM((16, 1536, 256), BF16),
            pltpu.VMEM((16, 1536, 256), BF16),
            pltpu.VMEM((16, 6, 256, 256), BF16),
            pltpu.VMEM((512, 256), BF16),
            pltpu.VMEM((512, 256), BF16),
            dma((4,)),
            dma((16,)),
            dma((16,)),
            dma((16,)),
            dma((16,)),
            dma((2, 3)),
            dma((2, 3)),
            dma((2, 4)),
            dma((2, 4)),
        ],
        compiler_params=pltpu.CompilerParams(
            collective_id=0, has_side_effects=True, vmem_limit_bytes=67043328
        ),
        cost_estimate=pl.CostEstimate(flops=11_000_000_000, bytes_accessed=28_000_000, transcendentals=0),
        name="spokes",
    )(image, deapodization, deapodization, offsets, cross_weight[0], x_weight[0], tz, ty, tx)
    return samples[None]


def solution(mesh):
    return jax.shard_map(
        per_device,
        mesh=mesh,
        in_specs=(
            P(None, "wide", "narrow", None),
            P(),
            P(("wide", "narrow"), None),
            P(("wide", "narrow"), None, None, None),
            P(("wide", "narrow"), None, None, None),
        ),
        out_specs=P(("wide", "narrow"), None, None, None),
        check_vma=False,
    )
```

time: 235 us -> 45.6 us (0.19)
  the two profiles are of different devices: /device:TPU:0 before, /device:TPU:1 now
where the time goes in v1:
time: 45.6 us; the launch traced here: 45.4 us
  Pallas kernels  43.8 us (96%)
  local copies, waits for them, and re-layouts  1.62 us (4%)
    pallas_call x1, Pallas kernels, per_device(): pl.pallas_call(kernel, out_shape=jax.ShapeDtypeStruct((16, 2, 1536), F32)...  43.8 us
    unnamed x1, local copies, waits for them, and re-layouts  1.62 us

profile of v1, /device:TPU:1, one launch (start us, length us, event | category | flops | bytes accessed | tf_op | source)
XLA Modules:
  0.0 45.4 jit_solution(16603138058834162230)
XLA Ops:
  0.0 43.8 %spokes.1 = f32[16,2,1536]{2,1,0:T(2,128)} custom-call(bf16[2,16,32,256]{3,2,1,0:T(8,128)(2,1)} %img_h.1, f32[3,256]{1,0:T(4,128)} %deap_s.1, f32[3,256]{1,0:T(4,128)} %deap_s.1, s32[1,16]{1,0:T(1,128)} %off_s.1, bf16[16,1536,256]{2,1,0:T(8,128)(2,1)} %bitcast.4, bf16[16,1536,256]{2,1,0:T(8,128)(2,1)} %bitcast.5, bf16[2,256,128]{2,1,0:T(8,128)(2,1)} %constant.6.clone.tz_h, ...), custom_call_target="tpu_custom_call" | custom-call | flops 11000000512 | bytes 28000000 | tf_op jit(solution)/shard_map/spokes/pallas_call | solution.py:333
  43.8 1.6 %copy.10 = f32[1,16,2,1536]{3,2,1,0:T(2,128)} copy(f32[1,16,2,1536]{3,2,1,0:T(2,128)} %bitcast.3) | data formatting | bytes 393216

commit v2 on v1

--- a/solution.py
+++ b/solution.py
@@ -121,6 +121,28 @@
     lax.fori_loop(0, 16, start_xw, 0)
     lax.fori_loop(0, 16, start_cw, 0)
 
+    ins[2].wait()
+    tyf[0, :, 0:256] = ty[0]
+    tyf[0, :, 256:512] = ty[1]
+    tyf[1, :, 0:256] = -ty[1]
+    tyf[1, :, 256:512] = ty[0]
+    ins[3].wait()
+
+    place = lax.broadcasted_iota(jnp.int32, (8, 256), 1)
+    place = (
+        ((place >> 6) & 1) * 128 + ((place >> 4) & 3) * 32 + (place >> 7) * 16 + (place & 15) - 128
+    )
+
+    def windows(s, _):
+        phase = (place * off_s[0, s]) & 511
+        angle = phase.astype(F32) * (2.0 * math.pi / 512)
+        cosine, sine = jnp.cos(angle)[0:1], jnp.sin(angle)[0:1]
+        twin[s, 0] = (tx[0] * cosine - tx[1] * sine).astype(BF16)
+        twin[s, 1] = (tx[1] * cosine + tx[0] * sine).astype(BF16)
+        return 0
+
+    lax.fori_loop(0, 16, windows, 0)
+
     pl.semaphore_wait(barrier, 18)
 
     def piece(d, src):
@@ -140,28 +162,6 @@
     lax.fori_loop(1, 16, send_piece, 0)
     blk[xh, :, pl.ds(pl.multiple_of(narrow * 32, 32), 32), :] = send[narrow]
 
-    ins[2].wait()
-    tyf[0, :, 0:256] = ty[0]
-    tyf[0, :, 256:512] = ty[1]
-    tyf[1, :, 0:256] = -ty[1]
-    tyf[1, :, 256:512] = ty[0]
-    ins[3].wait()
-
-    place = lax.broadcasted_iota(jnp.int32, (8, 256), 1)
-    place = (
-        ((place >> 6) & 1) * 128 + ((place >> 4) & 3) * 32 + (place >> 7) * 16 + (place & 15) - 128
-    )
-
-    def windows(s, _):
-        phase = (place * off_s[0, s]) & 511
-        angle = phase.astype(F32) * (2.0 * math.pi / 512)
-        cosine, sine = jnp.cos(angle)[0:1], jnp.sin(angle)[0:1]
-        twin[s, 0] = (tx[0] * cosine - tx[1] * sine).astype(BF16)
-        twin[s, 1] = (tx[1] * cosine + tx[0] * sine).astype(BF16)
-        return 0
-
-    lax.fori_loop(0, 16, windows, 0)
-
     def transpose_slabs(first, last):
         def one(s, _):
             xw_copy(s).wait()
@@ -171,6 +171,8 @@
 
         lax.fori_loop(first, last, one, 0)
 
+    transpose_slabs(0, 7)
+
     def got_piece(i, _):
         piece(me, (me + i) % 16).wait_recv()
         return 0
@@ -181,63 +183,66 @@
     band[0, y, core] = jnp.concatenate([b0[:, :64], b1[:, :64]], axis=1)
     band[1, y, core] = jnp.concatenate([b0[:, 64:], b1[:, 64:]], axis=1)
 
-    def ring(kg, kind, slot, step):
+    def ring(chunk, kind, slot, step):
+        part = band.at[chunk // 2, (y + slot) % 4, core, pl.ds((chunk % 2) * 256, 256), :]
         return pltpu.make_async_remote_copy(
-            src_ref=band.at[kg, (y + slot) % 4, core],
-            dst_ref=band.at[kg, (y + slot) % 4, core],
-            send_sem=s2.at[kg, kind],
-            recv_sem=r2.at[kg, kind],
+            src_ref=part,
+            dst_ref=part,
+            send_sem=s2.at[chunk, kind],
+            recv_sem=r2.at[chunk, kind],
             device_id=at_y(step),
             device_id_type=MESH,
         )
 
-    def got_ring(kg, kind, slot):
+    def across(chunk, slot, side):
+        part = band.at[chunk // 2, (y + slot) % 4, side, pl.ds((chunk % 2) * 256, 256), :]
         return pltpu.make_async_remote_copy(
-            src_ref=band.at[kg, (y + slot) % 4, core],
-            dst_ref=band.at[kg, (y + slot) % 4, core],
-            send_sem=s2.at[kg, kind],
-            recv_sem=r2.at[kg, kind],
-            device_id=at_y(1),
-            device_id_type=MESH,
-        )
-
-    def across(kg, slot, side):
-        return pltpu.make_async_remote_copy(
-            src_ref=band.at[kg, (y + slot) % 4, side],
-            dst_ref=band.at[kg, (y + slot) % 4, side],
-            send_sem=s3.at[kg, slot],
-            recv_sem=r3.at[kg, slot],
+            src_ref=part,
+            dst_ref=part,
+            send_sem=s3.at[chunk, slot],
+            recv_sem=r3.at[chunk, slot],
             device_id=other,
             device_id_type=MESH,
         )
 
-    ring(0, 0, 0, 1).start()
-    ring(0, 1, 0, 3).start()
+    def from_below(chunk):
+        ring(chunk, 0, 3, 1).wait_recv()
+        if chunk < 2:
+            ring(chunk, 2, 3, 1).start()
+        across(chunk, 3, core).start()
+
+    def from_above(chunk):
+        ring(chunk, 1, 1, 3).wait_recv()
+        if chunk >= 2:
+            ring(chunk, 2, 1, 3).start()
+        across(chunk, 1, core).start()
+
+    def from_far(chunk):
+        ring(chunk, 2, 2, 1).wait_recv()
+        across(chunk, 2, core).start()
+
+    for up, down in ((0, 2), (1, 3), (2, 0)):
+        ring(up, 0, 0, 1).start()
+        ring(down, 1, 0, 3).start()
     ring(1, 1, 0, 3).start()
-    across(0, 0, core).start()
-    across(1, 0, core).start()
-
-    transpose_slabs(0, 5)
-
-    got_ring(0, 0, 3).wait_recv()
-    ring(0, 2, 3, 1).start()
-    ring(1, 0, 0, 1).start()
-    across(0, 3, core).start()
-    got_ring(0, 1, 1).wait_recv()
-    across(0, 1, core).start()
-
-    transpose_slabs(5, 11)
-
-    got_ring(1, 1, 1).wait_recv()
-    ring(1, 2, 1, 3).start()
-    across(1, 1, core).start()
-    got_ring(0, 2, 2).wait_recv()
-    across(0, 2, core).start()
-
-    transpose_slabs(11, 16)
-
-    got_ring(1, 0, 3).wait_recv()
-    across(1, 3, core).start()
+    for chunk in range(4):
+        across(chunk, 0, core).start()
+
+    transpose_slabs(7, 12)
+    from_below(0)
+    from_above(2)
+    transpose_slabs(12, 14)
+    from_below(1)
+    ring(3, 0, 0, 1).start()
+    from_above(3)
+    transpose_slabs(14, 15)
+    from_below(2)
+    from_above(0)
+    transpose_slabs(15, 16)
+    from_above(1)
+    from_far(0)
+    from_far(1)
+    from_far(2)
 
     def lines(kg):
         lane_b = lax.broadcasted_iota(jnp.int32, (512, 128), 1)
@@ -264,13 +269,15 @@
                             s * 32 : (s + 1) * 32, t * 128 : (t + 1) * 128
                         ]
 
-    for slot in range(4):
-        across(0, slot, 1 - core).wait_recv()
+    for chunk in range(2):
+        for slot in range(4):
+            across(chunk, slot, 1 - core).wait_recv()
     lines(0)
-    got_ring(1, 2, 2).wait_recv()
-    across(1, 2, core).start()
-    for slot in range(4):
-        across(1, slot, 1 - core).wait_recv()
+    from_below(3)
+    from_far(3)
+    for chunk in range(2, 4):
+        for slot in range(4):
+            across(chunk, slot, 1 - core).wait_recv()
     lines(1)
 
     def got_cw(s, _):
@@ -299,29 +306,28 @@
             out[s, 1:2, here] = jnp.sum(part[256:] * gain, axis=0, keepdims=True)
 
     to_window(0, win_a)
-
-    def pair(i, _):
-        s = i * 2
-        to_window(s + 1, win_b)
-        to_samples(s, win_a)
-        to_window((s + 2) % 16, win_a)
-        to_samples(s + 1, win_b)
-        return 0
-
-    lax.fori_loop(0, 8, pair, 0)
+    wins = (win_a, win_b)
+
+    def group(i, _):
+        for u in range(8):
+            s = i * 8 + u
+            to_window((s + 1) % 16, wins[(u + 1) % 2])
+            to_samples(s, wins[u % 2])
+        return 0
+
+    lax.fori_loop(0, 2, group, 0)
 
     def sent(i, _):
         piece((me + i) % 16, me).wait_send()
         return 0
 
     lax.fori_loop(1, 16, sent, 0)
-    for kg in range(2):
-        ring(kg, 0, 0, 1).wait_send()
-        ring(kg, 1, 0, 3).wait_send()
+    for chunk in range(4):
+        ring(chunk, 0, 0, 1).wait_send()
+        ring(chunk, 1, 0, 3).wait_send()
+        ring(chunk, 2, 3, 1).wait_send()
         for slot in range(4):
-            across(kg, slot, core).wait_send()
-    ring(0, 2, 3, 1).wait_send()
-    ring(1, 2, 1, 3).wait_send()
+            across(chunk, slot, core).wait_send()
 
 
 def per_device(image, deapodization, offsets, cross_weight, x_weight):
@@ -357,10 +363,10 @@
             dma((16,)),
             dma((16,)),
             dma((16,)),
-            dma((2, 3)),
-            dma((2, 3)),
-            dma((2, 4)),
-            dma((2, 4)),
+            dma((4, 3)),
+            dma((4, 3)),
+            dma((4, 4)),
+            dma((4, 4)),
         ],
         compiler_params=pltpu.CompilerParams(
             collective_id=0, has_side_effects=True, vmem_limit_bytes=67043328

time: 45.6 us -> 44.3 us (0.971)
  Pallas kernels: 43.8 us -> 42.5 us
    pallas_call x1, Pallas kernels: 43.8 us -> 42.5 us  [per_device(): pl.pallas_call(kernel, out_shape=jax.ShapeDtypeStruct((16, 2, 1536), F32)...]
where the time goes in v2:
time: 44.3 us; the launch traced here: 44.1 us
  Pallas kernels  42.5 us (96%)
  local copies, waits for them, and re-layouts  1.62 us (4%)
    pallas_call x1, Pallas kernels, per_device(): pl.pallas_call(kernel, out_shape=jax.ShapeDtypeStruct((16, 2, 1536), F32)...  42.5 us
    unnamed x1, local copies, waits for them, and re-layouts  1.62 us

profile of v2, /device:TPU:1, one launch (start us, length us, event | category | flops | bytes accessed | tf_op | source)
XLA Modules:
  0.0 44.1 jit_solution(14633467207981779748)
XLA Ops:
  0.0 42.5 %spokes.1 = f32[16,2,1536]{2,1,0:T(2,128)} custom-call(bf16[2,16,32,256]{3,2,1,0:T(8,128)(2,1)} %img_h.1, f32[3,256]{1,0:T(4,128)} %deap_s.1, f32[3,256]{1,0:T(4,128)} %deap_s.1, s32[1,16]{1,0:T(1,128)} %off_s.1, bf16[16,1536,256]{2,1,0:T(8,128)(2,1)} %bitcast.4, bf16[16,1536,256]{2,1,0:T(8,128)(2,1)} %bitcast.5, bf16[2,256,128]{2,1,0:T(8,128)(2,1)} %constant.6.clone.tz_h, ...), custom_call_target="tpu_custom_call" | custom-call | flops 11000000512 | bytes 28000000 | tf_op jit(solution)/shard_map/spokes/pallas_call | solution.py:339
  42.5 1.6 %copy.10 = f32[1,16,2,1536]{3,2,1,0:T(2,128)} copy(f32[1,16,2,1536]{3,2,1,0:T(2,128)} %bitcast.3) | data formatting | bytes 393216

commit v3 on v2

--- a/solution.py
+++ b/solution.py
@@ -34,14 +34,15 @@
     tz[0, :, :, 1], tz[1, :, :, 1] = -sin_t, cos_t
     tz = tz.reshape(2, 256, 128)
     cosine, sine = trig(np.arange(512) - 256, position)
-    ty = np.stack([cosine, sine])
-    tx = ty[:, :256].reshape(2, 256, 2, 4, 2, 16).transpose(0, 1, 4, 2, 3, 5).reshape(2, 256, 256)
+    ty = np.concatenate([cosine, sine], axis=1)
+    tx = np.stack([cosine, sine])[:, :256].reshape(2, 256, 2, 4, 2, 16)
+    tx = tx.transpose(0, 1, 3, 4, 2, 5).reshape(2, 256, 256)
     return tz.astype(ml_dtypes.bfloat16), ty.astype(ml_dtypes.bfloat16), tx.astype(np.float32)
 
 
 def kernel(
     img_h, deap, deap_s, off_s, cw_h, xw_h, tz_h, ty_h, tx_h, out,
-    img, tz, ty, tx, dyz, send, blk, band, tyf, twin, col, cw, xw, xwt, win_a, win_b,
+    img, tz, ty, tx, dyz, send, blk, band, mix, turn, twin, acc, col, cw, xw, xwt, win_a, win_b,
     in_sem, cw_sem, xw_sem, s1, r1, s2, r2, s3, r3,
 ):
     wide = lax.axis_index("wide")
@@ -69,7 +70,7 @@
         copy.start()
 
     def xw_copy(s):
-        return pltpu.make_async_copy(xw_h.at[s], xw.at[s], xw_sem.at[s])
+        return pltpu.make_async_copy(xw_h.at[s], xw.at[s % 8], xw_sem.at[s])
 
     def cw_copy(s):
         return pltpu.make_async_copy(cw_h.at[s], cw.at[s], cw_sem.at[s])
@@ -81,7 +82,10 @@
         return 0
 
     lax.fori_loop(1, 16, greet, 0)
-    for target in (at_y(1), at_y(3), other):
+    def diagonal(step):
+        return {"wide": xh * 8 + ((y + step) % 4) * 2 + (1 - core), "narrow": narrow}
+
+    for target in (at_y(1), at_y(3), other, diagonal(1), diagonal(3)):
         pl.semaphore_signal(barrier, inc=1, device_id=target, device_id_type=MESH)
 
     dz = deap[2:3, :]
@@ -118,32 +122,66 @@
         cw_copy(s).start()
         return 0
 
-    lax.fori_loop(0, 16, start_xw, 0)
+    lax.fori_loop(0, 8, start_xw, 0)
     lax.fori_loop(0, 16, start_cw, 0)
 
+    row = lax.broadcasted_iota(jnp.int32, (512, 512), 0)
+    goal = (
+        ((row >> 4) & 3) * 128 + (row >> 8) * 64 + ((row >> 7) & 1) * 32 + ((row >> 6) & 1) * 16
+    ) + (row & 15)
+    mix[...] = (goal == lax.broadcasted_iota(jnp.int32, (512, 512), 1)).astype(BF16)
+
     ins[2].wait()
-    tyf[0, :, 0:256] = ty[0]
-    tyf[0, :, 256:512] = ty[1]
-    tyf[1, :, 0:256] = -ty[1]
-    tyf[1, :, 256:512] = ty[0]
     ins[3].wait()
-
-    place = lax.broadcasted_iota(jnp.int32, (8, 256), 1)
+    low = lax.broadcasted_iota(jnp.int32, (256, 128), 1) < 64
+    shift = ((4 - y) % 4) * 64
+    cos_r, sin_r = pltpu.roll(tx[0], shift, 1), pltpu.roll(tx[1], shift, 1)
+    c0, c1, z0, z1 = cos_r[:, :128], cos_r[:, 128:], sin_r[:, :128], sin_r[:, 128:]
+
+    def swap(v):
+        return pltpu.roll(v, 64, 1)
+
+    turn[0, :, 0:128] = jnp.where(low, c0, swap(z0))
+    turn[1, :, 0:128] = jnp.where(low, -z0, swap(c0))
+    turn[0, :, 128:256] = jnp.where(low, swap(c0), z0)
+    turn[1, :, 128:256] = jnp.where(low, -swap(z0), c0)
+    turn[0, :, 256:384] = jnp.where(low, swap(c1), z1)
+    turn[1, :, 256:384] = jnp.where(low, -swap(z1), c1)
+    turn[0, :, 384:512] = jnp.where(low, c1, swap(z1))
+    turn[1, :, 384:512] = jnp.where(low, -z1, swap(c1))
+
+    place = lax.broadcasted_iota(jnp.int32, (8, 512), 1)
+    tile = place >> 7
+    away = jnp.where(tile < 2, tile, 5 - tile)
     place = (
-        ((place >> 6) & 1) * 128 + ((place >> 4) & 3) * 32 + (place >> 7) * 16 + (place & 15) - 128
+        ((place >> 4) & 1) * 128 + ((y + away) & 3) * 32 + ((place >> 5) & 1) * 16 + (place & 15) - 128
     )
 
     def windows(s, _):
         phase = (place * off_s[0, s]) & 511
         angle = phase.astype(F32) * (2.0 * math.pi / 512)
         cosine, sine = jnp.cos(angle)[0:1], jnp.sin(angle)[0:1]
-        twin[s, 0] = (tx[0] * cosine - tx[1] * sine).astype(BF16)
-        twin[s, 1] = (tx[1] * cosine + tx[0] * sine).astype(BF16)
-        return 0
-
-    lax.fori_loop(0, 16, windows, 0)
-
-    pl.semaphore_wait(barrier, 18)
+        twin[s] = (turn[0] * cosine + turn[1] * sine).astype(BF16)
+        return 0
+
+    def transpose_slabs(first, last):
+        def one(s, _):
+            xw_copy(s).wait()
+            for j in range(6):
+                xwt[s, j] = xw[s % 8, j * 256 : (j + 1) * 256, :].T
+            return 0
+
+        def one_and_next(s, _):
+            one(s, 0)
+            xw_copy(s + 8).start()
+            return 0
+
+        if first < 8:
+            lax.fori_loop(first, min(last, 8), one_and_next, 0)
+        if last > 8:
+            lax.fori_loop(max(first, 8), last, one, 0)
+
+    pl.semaphore_wait(barrier, 20)
 
     def piece(d, src):
         return pltpu.make_async_remote_copy(
@@ -162,16 +200,8 @@
     lax.fori_loop(1, 16, send_piece, 0)
     blk[xh, :, pl.ds(pl.multiple_of(narrow * 32, 32), 32), :] = send[narrow]
 
-    def transpose_slabs(first, last):
-        def one(s, _):
-            xw_copy(s).wait()
-            for j in range(6):
-                xwt[s, j] = xw[s, j * 256 : (j + 1) * 256, :].T
-            return 0
-
-        lax.fori_loop(first, last, one, 0)
-
-    transpose_slabs(0, 7)
+    lax.fori_loop(0, 16, windows, 0)
+    transpose_slabs(0, 6)
 
     def got_piece(i, _):
         piece(me, (me + i) % 16).wait_recv()
@@ -205,96 +235,99 @@
             device_id_type=MESH,
         )
 
+    def pass_on(chunk, slot, step):
+        part = band.at[chunk // 2, (y + slot) % 4, core, pl.ds((chunk % 2) * 256, 256), :]
+        return pltpu.make_async_remote_copy(
+            src_ref=part,
+            dst_ref=part,
+            send_sem=s3.at[chunk, 2],
+            recv_sem=r3.at[chunk, 2],
+            device_id=diagonal(step),
+            device_id_type=MESH,
+        )
+
     def from_below(chunk):
         ring(chunk, 0, 3, 1).wait_recv()
         if chunk < 2:
             ring(chunk, 2, 3, 1).start()
+            pass_on(chunk, 3, 1).start()
         across(chunk, 3, core).start()
 
     def from_above(chunk):
         ring(chunk, 1, 1, 3).wait_recv()
         if chunk >= 2:
             ring(chunk, 2, 1, 3).start()
+            pass_on(chunk, 1, 3).start()
         across(chunk, 1, core).start()
 
     def from_far(chunk):
         ring(chunk, 2, 2, 1).wait_recv()
-        across(chunk, 2, core).start()
-
-    for up, down in ((0, 2), (1, 3), (2, 0)):
+
+    for up, down in ((0, 2), (1, 3), (2, 0), (3, 1)):
         ring(up, 0, 0, 1).start()
         ring(down, 1, 0, 3).start()
-    ring(1, 1, 0, 3).start()
     for chunk in range(4):
         across(chunk, 0, core).start()
 
-    transpose_slabs(7, 12)
-    from_below(0)
-    from_above(2)
-    transpose_slabs(12, 14)
-    from_below(1)
-    ring(3, 0, 0, 1).start()
-    from_above(3)
-    transpose_slabs(14, 15)
-    from_below(2)
-    from_above(0)
-    transpose_slabs(15, 16)
-    from_above(1)
-    from_far(0)
-    from_far(1)
-    from_far(2)
-
-    def lines(kg):
-        lane_b = lax.broadcasted_iota(jnp.int32, (512, 128), 1)
-        sides = []
-        for side in range(2):
-            rows = [band[kg, i, side].astype(F32) for i in range(4)]
-            for b in range(2):
-                step, shift = 1 << b, 16 << b
-                low = (lane_b & shift) == 0
-                for i in range(4):
-                    if i & step:
-                        continue
-                    a0, a1 = rows[i], rows[i + step]
-                    rows[i] = jnp.where(low, a0, pltpu.roll(a1, shift, 1))
-                    rows[i + step] = jnp.where(low, pltpu.roll(a0, 128 - shift, 1), a1)
-            sides.append([r.astype(BF16) for r in rows])
-        for k in range(4):
-            data = jnp.concatenate([sides[0][k], sides[1][k]], axis=1)
-            for c in range(2):
-                line = lax.dot_general(tyf[c], data, NN, preferred_element_type=F32)
+    transpose_slabs(6, 12)
+
+    def from_other(slot):
+        for chunk in range(4):
+            across(chunk, slot, 1 - core).wait_recv()
+
+    def lines(slot, buf):
+        line_y = (y + slot) % 4
+        ty_all = ty[...]
+        for kg in range(2):
+            d0, d1 = band[kg, line_y, 0], band[kg, line_y, 1]
+            real = jnp.concatenate([d0[:256], d1[:256]], axis=1)
+            imag = jnp.concatenate([d0[256:], d1[256:]], axis=1)
+            top = jnp.concatenate([real, imag], axis=1)
+            low_half = jnp.concatenate([imag, -real], axis=1)
+            data = jnp.concatenate([top, low_half], axis=0)
+            data = lax.dot_general(data, mix[...], NN, preferred_element_type=F32).astype(BF16)
+            line = lax.dot_general(ty_all, data, NN, preferred_element_type=F32)
+            for k in range(4):
                 for s in range(16):
-                    for t in range(2):
-                        col[s, c, t, pl.ds(kg * 4 + k, 32, stride=8), :] = line[
-                            s * 32 : (s + 1) * 32, t * 128 : (t + 1) * 128
-                        ]
-
-    for chunk in range(2):
-        for slot in range(4):
-            across(chunk, slot, 1 - core).wait_recv()
-    lines(0)
-    from_below(3)
-    from_far(3)
-    for chunk in range(2, 4):
-        for slot in range(4):
-            across(chunk, slot, 1 - core).wait_recv()
-    lines(1)
-
-    def got_cw(s, _):
-        cw_copy(s).wait()
-        return 0
-
-    lax.fori_loop(0, 16, got_cw, 0)
+                    col[buf, s, pl.ds(kg * 4 + k, 32, stride=8), :] = line[
+                        s * 32 : (s + 1) * 32, k * 128 : (k + 1) * 128
+                    ]
+
+    def loop(work, first, last, unroll):
+        def body(i, _):
+            for u in range(unroll):
+                work(first + i * unroll + u)
+            return 0
+
+        lax.fori_loop(0, (last - first) // unroll, body, 0)
+
+    def turned(t):
+        t = swap(t)
+        return jnp.where(low, t, -t)
+
+    def window_part(s, bufs, lanes):
+        lines_of = [col[b, s] for b in bufs]
+        table = twin[s, :, lanes]
+        parts = []
+        for form in (lambda t: t, turned):
+            source = jnp.concatenate([form(t) for t in lines_of], axis=1).astype(BF16)
+            parts.append(lax.dot_general(table, source, NT, preferred_element_type=F32))
+        return parts
+
+    def own_window(s):
+        real, imag = window_part(s, (0,), slice(0, 128))
+        acc[s, 0:256] = real
+        acc[s, 256:512] = imag
+
+    def near_window(s):
+        real, imag = window_part(s, (1, 2), slice(128, 384))
+        acc[s, 0:256] += real
+        acc[s, 256:512] += imag
 
     def to_window(s, win):
-        cosine, sine = twin[s, 0], twin[s, 1]
-        real = jnp.concatenate([cosine, sine], axis=1)
-        imag = jnp.concatenate([-sine, cosine], axis=1)
-        source = jnp.concatenate(
-            [col[s, c, t].astype(BF16) for c in range(2) for t in range(2)], axis=1
-        )
-        win[0:256] = lax.dot_general(real, source, NT, preferred_element_type=F32).astype(BF16)
-        win[256:512] = lax.dot_general(imag, source, NT, preferred_element_type=F32).astype(BF16)
+        real, imag = window_part(s, (0,), slice(384, 512))
+        win[0:256] = (acc[s, 0:256] + real).astype(BF16)
+        win[256:512] = (acc[s, 256:512] + imag).astype(BF16)
 
     def to_samples(s, win):
         for j in range(6):
@@ -305,17 +338,42 @@
             out[s, 0:1, here] = jnp.sum(part[:256] * gain, axis=0, keepdims=True)
             out[s, 1:2, here] = jnp.sum(part[256:] * gain, axis=0, keepdims=True)
 
+    from_other(0)
+    lines(0, 0)
+    from_below(0)
+    from_above(2)
+    transpose_slabs(12, 16)
+    from_below(1)
+    from_above(3)
+    loop(own_window, 0, 16, 4)
+    from_below(2)
+    from_above(0)
+    from_below(3)
+    from_above(1)
+    from_other(3)
+    lines(3, 2)
+    from_other(1)
+    lines(1, 1)
+    loop(near_window, 0, 16, 4)
+
+    def got_cw(s, _):
+        cw_copy(s).wait()
+        return 0
+
+    lax.fori_loop(0, 16, got_cw, 0)
+    from_far(0)
+    from_far(2)
+    from_far(1)
+    from_far(3)
+    from_other(2)
+    lines(2, 0)
     to_window(0, win_a)
     wins = (win_a, win_b)
 
-    def group(i, _):
-        for u in range(8):
-            s = i * 8 + u
-            to_window((s + 1) % 16, wins[(u + 1) % 2])
-            to_samples(s, wins[u % 2])
-        return 0
-
-    lax.fori_loop(0, 2, group, 0)
+    for s in range(16):
+        if s < 15:
+            to_window(s + 1, wins[(s + 1) % 2])
+        to_samples(s, wins[s % 2])
 
     def sent(i, _):
         piece((me + i) % 16, me).wait_send()
@@ -344,17 +402,19 @@
         scratch_shapes=[
             pltpu.VMEM((2, 16, 32, 256), BF16),
             pltpu.VMEM((2, 256, 128), BF16),
-            pltpu.VMEM((2, 512, 256), BF16),
+            pltpu.VMEM((512, 512), BF16),
             pltpu.VMEM((2, 256, 256), F32),
             pltpu.VMEM((32, 256), F32),
             pltpu.VMEM((8, 2, 32, 128), BF16),
             pltpu.VMEM((2, 2, 256, 128), BF16),
             pltpu.VMEM((2, 4, 2, 512, 128), BF16),
-            pltpu.VMEM((2, 512, 512), BF16),
-            pltpu.VMEM((16, 2, 256, 256), BF16),
-            pltpu.VMEM((16, 2, 2, 256, 128), F32),
+            pltpu.VMEM((512, 512), BF16),
+            pltpu.VMEM((2, 256, 512), F32),
+            pltpu.VMEM((16, 256, 512), BF16),
+            pltpu.VMEM((16, 512, 256), F32),
+            pltpu.VMEM((3, 16, 256, 128), F32),
             pltpu.VMEM((16, 1536, 256), BF16),
-            pltpu.VMEM((16, 1536, 256), BF16),
+            pltpu.VMEM((8, 1536, 256), BF16),
             pltpu.VMEM((16, 6, 256, 256), BF16),
             pltpu.VMEM((512, 256), BF16),
             pltpu.VMEM((512, 256), BF16),

time: 44.3 us -> 42.6 us (0.962)
  Pallas kernels: 42.5 us -> 40.8 us
    pallas_call x1, Pallas kernels: 42.5 us -> 40.8 us  [per_device(): pl.pallas_call(kernel, out_shape=jax.ShapeDtypeStruct((16, 2, 1536), F32)...]
where the time goes in v3:
time: 42.6 us; the launch traced here: 42.4 us
  Pallas kernels  40.8 us (96%)
  local copies, waits for them, and re-layouts  1.62 us (4%)
    pallas_call x1, Pallas kernels, per_device(): pl.pallas_call(kernel, out_shape=jax.ShapeDtypeStruct((16, 2, 1536), F32)...  40.8 us
    unnamed x1, local copies, waits for them, and re-layouts  1.62 us

profile of v3, /device:TPU:1, one launch (start us, length us, event | category | flops | bytes accessed | tf_op | source)
XLA Modules:
  0.0 42.4 jit_solution(8265809840840566169)
XLA Ops:
  0.0 40.8 %spokes.1 = f32[16,2,1536]{2,1,0:T(2,128)} custom-call(bf16[2,16,32,256]{3,2,1,0:T(8,128)(2,1)} %img_h.1, f32[3,256]{1,0:T(4,128)} %deap_s.1, f32[3,256]{1,0:T(4,128)} %deap_s.1, s32[1,16]{1,0:T(1,128)} %off_s.1, bf16[16,1536,256]{2,1,0:T(8,128)(2,1)} %bitcast.4, bf16[16,1536,256]{2,1,0:T(8,128)(2,1)} %bitcast.5, bf16[2,256,128]{2,1,0:T(8,128)(2,1)} %constant.6.clone.tz_h, ...), custom_call_target="tpu_custom_call" | custom-call | flops 11000000512 | bytes 28000000 | tf_op jit(solution)/shard_map/spokes/pallas_call | solution.py:397
  40.8 1.6 %copy.10 = f32[1,16,2,1536]{3,2,1,0:T(2,128)} copy(f32[1,16,2,1536]{3,2,1,0:T(2,128)} %bitcast.3) | data formatting | bytes 393216
